TPU v7x, 32 devices: a whole 2x2x4 slice. The times are simulated.
32 devices in a mesh: seq: 16 (over z, y, x), tp: 2 (over core).
Axes of the slice: x: 2, y: 2, z: 4, core: 2. Of those that a mesh axis runs over, the one named last changes fastest.
Arguments:
- tokens: bfloat16 [8192, 2048], P('seq', 'tp'), may hold values from -6 to 6
- ln_gain: bfloat16 [2048], replicated, may hold values from 0.5 to 4.1
- w_qkv: bfloat16 [3, 2048, 2048], P(None, None, 'tp'), may hold values from -0.15467961 to 0.15467961
- w_out: bfloat16 [2048, 2048], P('tp'), may hold values from -0.1875 to 0.1875
Outputs:
- mixed: bfloat16 [8192, 2048], P('seq', 'tp')
All inputs are finite; a program needn't handle non-finite values.
Results may differ from a plain program's by a relative error of at most 0.011.
Values may be sent and summed in bfloat16 or wider, within the bound.
A program may use at most 256 MiB of HBM per device.

v0:
```python
import jax
import jax.numpy as jnp
from jax import lax
from jax.sharding import PartitionSpec as P

HEAD_DIM = 128


def attend_block(totals, queries, block_kv, factor):
    running, denoms, accum = totals
    heads_here = queries.shape[1]
    keys_part = block_kv[0].reshape(block_kv.shape[1], heads_here, queries.shape[2])
    vals_part = block_kv[1].reshape(block_kv.shape[1], heads_here, queries.shape[2])
    scores = (
        jnp.einsum("thc,shc->ths", queries, keys_part, preferred_element_type=jnp.float32) * factor
    )
    highest = jnp.maximum(running, jnp.max(scores, axis=2))
    expon = jnp.exp(scores - highest[:, :, None])
    denoms = jnp.sum(expon, axis=2)
    weights = expon.astype(jnp.bfloat16)
    accum = jnp.einsum("ths,shc->thc", weights, vals_part, preferred_element_type=jnp.float32)
    return (highest, denoms, accum)


def start_totals(rows, heads_count):
    return (
        jnp.full((rows, heads_count), -1e30, jnp.float32),
        jnp.zeros((rows, heads_count), jnp.float32),
        jnp.zeros((rows, heads_count, HEAD_DIM), jnp.float32),
    )


def on_device(tokens, ln_gain, w_qkv, w_out):
    tok_rows = tokens.shape[0]
    whole = lax.all_gather(tokens, "tp", axis=1, tiled=True)
    values = whole.astype(jnp.float32)
    average = jnp.mean(values, axis=1, keepdims=True)
    second = jnp.mean(values * values, axis=1, keepdims=True)
    normed = (
        (values - average)
        * lax.rsqrt(second - average * average + 1e-06)
        * ln_gain.astype(jnp.float32)
    ).astype(jnp.bfloat16)
    projected = jnp.einsum("td,jdc->jtc", normed, w_qkv, preferred_element_type=jnp.float32).astype(
        jnp.bfloat16
    )
    heads_here = w_qkv.shape[2] // HEAD_DIM
    factor = HEAD_DIM ** (-0.5)
    queries = projected[0].reshape(tok_rows, heads_here, HEAD_DIM)
    keys_vals = projected[1:3]
    initial = start_totals(tok_rows, heads_here)
    final = attend_block(
        initial, queries, lax.all_gather(keys_vals, "seq", axis=1, tiled=True), factor
    )
    context = (
        (final[2] / final[1][:, :, None])
        .reshape(tok_rows, heads_here * HEAD_DIM)
        .astype(jnp.bfloat16)
    )
    summed = lax.psum_scatter(
        lax.dot_general(
            w_out, context, (((0,), (1,)), ((), ())), preferred_element_type=jnp.float32
        ).astype(jnp.bfloat16),
        "tp",
        scatter_dimension=0,
        tiled=True,
    ).astype(jnp.float32)
    return (tokens.astype(jnp.float32) + summed.T).astype(jnp.bfloat16)


def solution(mesh):
    in_specs = (P("seq", "tp"), P(), P(None, None, "tp"), P("tp", None))
    out_specs = P("seq", "tp")
    return jax.shard_map(
        on_device, mesh=mesh, in_specs=in_specs, out_specs=out_specs, check_vma=False
    )
```

profile of v0, /device:TPU:0, one launch (start us, length us, event | category | flops | bytes accessed | tf_op | source)
XLA Modules:
  0.0 599.8 jit_solution(8259866064880003707)
XLA Ops:
  6.5 0.0 all-gather.3.cloned.1.call-start
  6.5 0.7 all-gather.3.cloned.1.call-update
  7.3 0.0 all-gather.5.cloned.1.call-start
  7.3 0.7 convert_element_type.39
  8.0 14.2 %all-gather.3.cloned.1.call-done = bf16[512,2048]{1,0:T(8,128)(2,1)} async-done(((bf16[512,1024]{1,0:T(8,128)(2,1)}), bf16[512,2048]{1,0:T(8,128)(2,1)}) %all-gather.3.cloned.1.call-update) | async-done | bytes 2097168 | tf_op jit(solution)/shard_map/all_gather | solution.py:35
  22.2 2.3 convert_reduce_fusion
  24.5 10.5 %convert_bitcast_fusion = bf16[3,512,1024]{2,1,0:T(8,128)(2,1)S(1)} fusion(bf16[3,2048,1024]{2,1,0:T(8,128)(2,1)} %param.6, bf16[512,2048]{1,0:T(8,128)(2,1)} %all-gather.3.cloned.1.call-done, f32[2048]{0:T(1024)S(1)} %convert_element_type.39, f32[512]{0:T(512)S(1)} %get-tuple-element.10, f32[512]{0:T(512)S(1)} %get-tuple-element.9), kind=kOutput, calls=%fused_computation.16 | convolution fusion | flops 6449266688 | bytes 17838080 | tf_op jit(solution)/shard_map/td,jdc->jtc/dot_general | solution.py:44
  35.0 1.5 slice.16
  36.5 0.0 all-gather.5.cloned.1.call-update
  36.5 0.2 reduce-scatter.2.cloned.1.call-start
  36.7 0.1 slice_bitcast_fusion.1
  36.8 0.3 copy.12
  37.1 350.9 %all-gather.5.cloned.1.call-done = bf16[2,8192,1024]{2,1,0:T(8,128)(2,1)} async-done(((bf16[2,512,1024]{2,1,0:T(8,128)(2,1)}), bf16[2,8192,1024]{2,1,0:T(8,128)(2,1)}) %all-gather.5.cloned.1.call-update) | async-done | bytes 33554448 | tf_op jit(solution)/shard_map/all_gather | solution.py:53
  388.0 19.2 %slice_bitcast_fusion = (bf16[1024,8,8,128]{3,1,2,0:T(8,128)(2,1)S(1)}, bf16[1,8192,1024]{2,1,0:T(8,128)(2,1)}) fusion(bf16[2,8192,1024]{2,1,0:T(8,128)(2,1)} %all-gather.5.cloned.1.call-done), kind=kLoop, calls=%fused_computation.6 | loop fusion | bytes 67108864
  407.2 9.1 %copy.11 = bf16[1024,8,8,128]{3,2,1,0:T(8,128)(2,1)} copy(bf16[1024,8,8,128]{3,1,2,0:T(8,128)(2,1)S(1)} %get-tuple-element.7) | data formatting | bytes 33554432
  416.3 20.7 %copy.10 = bf16[1,8192,1024]{1,2,0:T(8,128)(2,1)} copy(bf16[1,8192,1024]{2,1,0:T(8,128)(2,1)} %get-tuple-element.8) | data formatting | bytes 33554432 | tf_op jit(solution)/shard_map/reshape;squeeze | solution.py:13
  437.0 50.1 %bitcast_reduce_fusion = (f32[512,8]{0,1:T(8,128)S(1)}, f32[8,8192,512]{2,1,0:T(8,128)}) fusion(bf16[512,8,128]{2,1,0:T(8,128)(2,1)S(1)} %bitcast.43, bf16[8192,8,128]{2,1,0:T(8,128)(2,1)} %bitcast.41), kind=kOutput, calls=%fused_computation.1 | convolution fusion | flops 8657039360 | bytes 152059904 | tf_op jit(solution)/shard_map/thc,shc->ths/dot_general | solution.py:15
  487.1 41.4 %fusion.1 = f32[512,8]{0,1:T(8,128)S(1)} fusion(f32[8,8192,512]{2,1,0:T(8,128)} %get-tuple-element.12, f32[512,8]{0,1:T(8,128)S(1)} %broadcast_maximum_fusion), kind=kLoop, calls=%fused_computation.3 | loop fusion | flops 100659200 | bytes 134250496 | tf_op jit(solution)/shard_map/reduce_sum | solution.py:19
  528.5 48.2 %fusion.15 = bf16[512,8,128]{0,2,1:T(8,128)(2,1)S(1)} fusion(bf16[8192,8,128]{0,2,1:T(8,128)(2,1)} %bitcast.42, f32[8,8192,512]{2,1,0:T(8,128)} %get-tuple-element.12, f32[512,8]{0,1:T(8,128)S(1)} %broadcast_maximum_fusion, f32[512,8]{0,1:T(8,128)S(1)} %fusion.1), kind=kOutput, calls=%fused_computation.23 | convolution fusion | flops 8691646464 | bytes 152076288 | tf_op jit(solution)/shard_map/ths,shc->thc/dot_general | solution.py:21
  576.7 0.0 copy-start
  576.7 6.0 %fusion.11 = bf16[2048,512]{0,1:T(8,128)(2,1)} fusion(bf16[512,1024]{0,1:T(8,128)(2,1)S(1)} %bitcast.44, bf16[1024,2048]{1,0:T(8,128)(2,1)} %param.7), kind=kOutput, calls=%fused_computation.18 | convolution fusion | flops 2148532224 | bytes 7340032 | tf_op jit(solution)/shard_map/dot_general | solution.py:61
  582.7 0.0 reduce-scatter.2.cloned.1.call-update
  582.8 8.0 %reduce-scatter.2.cloned.1.call-done = bf16[1024,512]{0,1:T(8,128)(2,1)} async-done(((bf16[2048,512]{0,1:T(8,128)(2,1)}), bf16[1024,512]{0,1:T(8,128)(2,1)}) %reduce-scatter.2.cloned.1.call-update) | async-done | bytes 1048592 | tf_op jit(solution)/shard_map/reduce_scatter | solution.py:60
  590.7 0.0 copy-done
  590.7 2.6 fusion.14
  (2 shorter events, 0.0 us)
Async XLA Ops:
  6.5 15.7 %all-gather.3.cloned.1.call-start = ((), (), s32[]{:S(2)}) async-start(), calls=%async_computation.1 | async-start | bytes 3145728 | tf_op jit(solution)/shard_map/all_gather | solution.py:35
  7.3 380.7 %all-gather.5.cloned.1.call-start = ((), (), s32[]{:S(2)}) async-start(), calls=%async_computation.2 | async-start | bytes 35651584 | tf_op jit(solution)/shard_map/all_gather | solution.py:53
  36.5 554.2 %reduce-scatter.2.cloned.1.call-start = ((), (), s32[]{:S(2)}) async-start(), calls=%async_computation.3 | async-start | bytes 3145728 | tf_op jit(solution)/shard_map/reduce_scatter | solution.py:60
  576.7 14.0 %copy-start = (bf16[512,1024]{1,0:T(8,128)(2,1)S(1)}, bf16[512,1024]{1,0:T(8,128)(2,1)}, u32[]{:S(2)}) copy-start(bf16[512,1024]{1,0:T(8,128)(2,1)} %param.4) | copy-start | bytes 3145732
Sparse Core Ops, SparseCore 0:
  8.9 13.2 all-gather.2
  36.6 351.2 all-gather.4
  582.9 7.7 reduce-scatter.1
where the time goes:
time: 601 us; the launch traced here: 600 us
  waiting for transfers between devices  374 us (62%)
  matrix products  115 us (19%)
  local copies, waits for them, and re-layouts  50.9 us (8%)
  other arithmetic  47 us (8%)
  between operations  13.2 us (2%)
    all_gather x1, waiting for transfers between devices, on_device(): lax.all_gather(keys_vals, 'seq', axis=1, tiled=True)  351 us
    dot_general x1, matrix products, attend_block(): jnp.einsum('thc,shc->ths', queries, keys_part, preferred_element_type=jnp...  50.1 us
    dot_general x1, matrix products, attend_block(): jnp.einsum('ths,shc->thc', weights, vals_part, preferred_element_type=jnp...  48.2 us
    reduce_sum x1, other arithmetic, attend_block(): denoms = jnp.sum(expon, axis=2)  41.4 us
    unnamed x6, local copies, waits for them, and re-layouts  28.7 us
    another operation x1, local copies, waits for them, and re-layouts, attend_block(): block_kv[1].reshape(block_kv.shape[1], heads_here, queries.shape[2])  20.7 us
    all_gather x1, waiting for transfers between devices, on_device(): whole = lax.all_gather(tokens, 'tp', axis=1, tiled=True)  14.2 us
  transfers between devices with their start and end apart: 3, of which 3 were waited for; matrix products, arithmetic and copies ran while one was open for 0% of the time, Pallas kernels for 0%

commit v1 on v0

--- a/solution.py
+++ b/solution.py
@@ -50,7 +50,7 @@
     keys_vals = projected[1:3]
     initial = start_totals(tok_rows, heads_here)
     final = attend_block(
-        initial, queries, lax.all_gather(keys_vals, "seq", axis=1, tiled=True), factor
+        initial, queries, jnp.concatenate(lax.all_gather(keys_vals, "seq"), axis=1), factor
     )
     context = (
         (final[2] / final[1][:, :, None])

time: 601 us -> 606 us (level)
    all_gather x0 -> x1, local copies, waits for them, and re-layouts: none -> 22.6 us  [on_device(): lax.all_gather(keys_vals, 'seq')]
    another operation x1 -> x0, local copies, waits for them, and re-layouts: 20.7 us -> none  [attend_block(): block_kv[1].reshape(block_kv.shape[1], heads_here, queries.shape[2])]
    slice x0 -> x1, local copies, waits for them, and re-layouts: none -> 12.7 us  [attend_block(): block_kv[1].reshape(block_kv.shape[1], heads_here, queries.shape[2])]
    unnamed x6, local copies, waits for them, and re-layouts: 28.7 us -> 18.6 us
where the time goes in v1:
time: 606 us; the launch traced here: 605 us
  waiting for transfers between devices  374 us (62%)
  matrix products  116 us (19%)
  local copies, waits for them, and re-layouts  55.4 us (9%)
  other arithmetic  47 us (8%)
  between operations  13.2 us (2%)
    all_gather x1, waiting for transfers between devices, on_device(): lax.all_gather(keys_vals, 'seq')  351 us
    dot_general x1, matrix products, attend_block(): jnp.einsum('thc,shc->ths', queries, keys_part, preferred_element_type=jnp...  50 us
    dot_general x1, matrix products, attend_block(): jnp.einsum('ths,shc->thc', weights, vals_part, preferred_element_type=jnp...  49.1 us
    reduce_sum x1, other arithmetic, attend_block(): denoms = jnp.sum(expon, axis=2)  41.4 us
    all_gather x1, local copies, waits for them, and re-layouts, on_device(): lax.all_gather(keys_vals, 'seq')  22.6 us
    unnamed x6, local copies, waits for them, and re-layouts  18.6 us
    all_gather x1, waiting for transfers between devices, on_device(): whole = lax.all_gather(tokens, 'tp', axis=1, tiled=True)  14.2 us
    slice x1, local copies, waits for them, and re-layouts, attend_block(): block_kv[1].reshape(block_kv.shape[1], heads_here, queries.shape[2])  12.7 us
  transfers between devices with their start and end apart: 3, of which 3 were waited for; matrix products, arithmetic and copies ran while one was open for 0% of the time, Pallas kernels for 0%

profile of v1, /device:TPU:0, one launch (start us, length us, event | category | flops | bytes accessed | tf_op | source)
XLA Modules:
  0.0 605.3 jit_solution(3589919115182919512)
XLA Ops:
  6.5 0.0 all-gather.4.cloned.1.call-start
  6.5 0.7 all-gather.4.cloned.1.call-update
  7.3 0.0 all-gather.6.cloned.1.call-start
  7.3 0.7 convert_element_type.39
  8.0 14.2 %all-gather.4.cloned.1.call-done = bf16[512,2048]{1,0:T(8,128)(2,1)} async-done(((bf16[512,1024]{1,0:T(8,128)(2,1)}), bf16[512,2048]{1,0:T(8,128)(2,1)}) %all-gather.4.cloned.1.call-update) | async-done | bytes 2097168 | tf_op jit(solution)/shard_map/all_gather | solution.py:35
  22.2 2.3 convert_reduce_fusion
  24.5 10.5 %convert_bitcast_fusion = bf16[3,512,1024]{2,1,0:T(8,128)(2,1)S(1)} fusion(bf16[3,2048,1024]{2,1,0:T(8,128)(2,1)} %param.6, bf16[512,2048]{1,0:T(8,128)(2,1)} %all-gather.4.cloned.1.call-done, f32[2048]{0:T(1024)S(1)} %convert_element_type.39, f32[512]{0:T(512)S(1)} %get-tuple-element.10, f32[512]{0:T(512)S(1)} %get-tuple-element.9), kind=kOutput, calls=%fused_computation.17 | convolution fusion | flops 6449266688 | bytes 17838080 | tf_op jit(solution)/shard_map/td,jdc->jtc/dot_general | solution.py:44
  35.0 1.5 slice.18
  36.5 0.0 all-gather.6.cloned.1.call-update
  36.5 0.2 reduce-scatter.2.cloned.1.call-start
  36.7 0.1 slice_bitcast_fusion
  36.8 0.3 copy.22
  37.1 351.0 %all-gather.6.cloned.1.call-done = bf16[32,512,1024]{2,1,0:T(8,128)(2,1)} async-done(((bf16[2,512,1024]{2,1,0:T(8,128)(2,1)}), bf16[32,512,1024]{2,1,0:T(8,128)(2,1)}) %all-gather.6.cloned.1.call-update) | async-done | bytes 33554448 | tf_op jit(solution)/shard_map/all_gather | solution.py:53
  388.1 22.6 %copy.36 = bf16[16,2,512,1024]{3,2,0,1:T(8,128)(2,1)} copy(bf16[16,2,512,1024]{3,2,1,0:T(8,128)(2,1)} %bitcast.51) | data formatting | bytes 67108864 | tf_op jit(solution)/shard_map/all_gather | solution.py:53
  410.7 12.7 %fusion.26 = (bf16[1,16,512,1024]{3,2,1,0:T(8,128)(2,1)S(1)}, bf16[1,16,512,1024]{3,2,1,0:T(8,128)(2,1)S(1)}) fusion(bf16[2,16,512,1024]{3,2,1,0:T(8,128)(2,1)} %bitcast.47), kind=kLoop, calls=%fused_computation.34 | loop fusion | bytes 67108864 | tf_op jit(solution)/shard_map/slice | solution.py:13
  423.4 9.1 %copy.20 = bf16[1024,8,8,128]{3,2,1,0:T(8,128)(2,1)} copy(bf16[1024,8,8,128]{3,1,2,0:T(8,128)(2,1)S(1)} %bitcast.50) | data formatting | bytes 33554432
  432.5 9.1 %copy.21 = bf16[1024,8,8,128]{3,2,1,0:T(8,128)(2,1)} copy(bf16[1024,8,8,128]{3,1,2,0:T(8,128)(2,1)S(1)} %bitcast.49) | data formatting | bytes 33554432
  441.6 50.0 %bitcast_reduce_fusion = (f32[512,8]{0,1:T(8,128)S(1)}, f32[8,8192,512]{2,1,0:T(8,128)}) fusion(bf16[512,8,128]{2,1,0:T(8,128)(2,1)S(1)} %bitcast.53, bf16[8192,8,128]{2,1,0:T(8,128)(2,1)} %bitcast.48), kind=kOutput, calls=%fused_computation.1 | convolution fusion | flops 8657039360 | bytes 152059904 | tf_op jit(solution)/shard_map/thc,shc->ths/dot_general | solution.py:15
  491.7 41.4 %fusion.1 = f32[512,8]{0,1:T(8,128)S(1)} fusion(f32[8,8192,512]{2,1,0:T(8,128)} %get-tuple-element.12, f32[512,8]{0,1:T(8,128)S(1)} %broadcast_maximum_fusion), kind=kLoop, calls=%fused_computation.3 | loop fusion | flops 100659200 | bytes 134250496 | tf_op jit(solution)/shard_map/reduce_sum | solution.py:19
  533.1 49.1 %fusion.16 = bf16[512,8,128]{0,2,1:T(8,128)(2,1)S(1)} fusion(f32[8,8192,512]{2,1,0:T(8,128)} %get-tuple-element.12, f32[512,8]{0,1:T(8,128)S(1)} %broadcast_maximum_fusion, bf16[8192,8,128]{2,1,0:T(8,128)(2,1)} %bitcast.52, f32[512,8]{0,1:T(8,128)S(1)} %fusion.1), kind=kOutput, calls=%fused_computation.24 | convolution fusion | flops 8691646464 | bytes 152076288 | tf_op jit(solution)/shard_map/ths,shc->thc/dot_general | solution.py:21
  582.2 0.0 copy-start
  582.2 6.0 fusion.12
  588.2 0.0 reduce-scatter.2.cloned.1.call-update
  588.3 8.0 %reduce-scatter.2.cloned.1.call-done = bf16[1024,512]{0,1:T(8,128)(2,1)} async-done(((bf16[2048,512]{0,1:T(8,128)(2,1)}), bf16[1024,512]{0,1:T(8,128)(2,1)}) %reduce-scatter.2.cloned.1.call-update) | async-done | bytes 1048592 | tf_op jit(solution)/shard_map/reduce_scatter | solution.py:60
  596.2 0.0 copy-done
  596.2 2.6 fusion.15
  (2 shorter events, 0.0 us)
Async XLA Ops:
  6.5 15.7 %all-gather.4.cloned.1.call-start = ((), (), s32[]{:S(2)}) async-start(), calls=%async_computation.1 | async-start | bytes 3145728 | tf_op jit(solution)/shard_map/all_gather | solution.py:35
  7.3 380.8 %all-gather.6.cloned.1.call-start = ((), (), s32[]{:S(2)}) async-start(), calls=%async_computation.3 | async-start | bytes 35651584 | tf_op jit(solution)/shard_map/all_gather | solution.py:53
  36.5 559.7 %reduce-scatter.2.cloned.1.call-start = ((), (), s32[]{:S(2)}) async-start(), calls=%async_computation.2 | async-start | bytes 3145728 | tf_op jit(solution)/shard_map/reduce_scatter | solution.py:60
  582.2 14.0 %copy-start = (bf16[512,1024]{1,0:T(8,128)(2,1)S(1)}, bf16[512,1024]{1,0:T(8,128)(2,1)}, u32[]{:S(2)}) copy-start(bf16[512,1024]{1,0:T(8,128)(2,1)} %param.4) | copy-start | bytes 3145732
Sparse Core Ops, SparseCore 0:
  8.9 13.2 all-gather.3
  36.6 351.4 all-gather.5
  588.4 7.7 reduce-scatter.1
